TPU v7x, 32 devices: a whole 2x2x4 slice. The times are simulated.
32 devices in a mesh: slab: 8 (over y, x, core), chan: 4 (over z).
Axes of the slice: x: 2, y: 2, z: 4, core: 2. Of those that a mesh axis runs over, the one named last changes fastest.
Arguments:
- features: bfloat16 [96, 16384], P('chan', 'slab'), may hold values from -1 to 3
- coords: bfloat16 [3, 16384], P(None, 'slab'), may hold values from 0 to 1
- send_rows: int32 [2, 8192], P(None, 'slab'), may hold values from 0 to 2047
- send_count: int32 [2, 8], P(None, 'slab'), may hold values from 1 to 1024, as said below
- neighbours: int32 [1024, 128], P('slab'), may hold values from 0 to 4095, as said below
- neighbour_count: int32 [1024], P('slab'), may hold values from 32 to 128
- geom_weight: bfloat16 [80, 6], replicated, may hold values from -3.5 to 3.5
- feat_weight: bfloat16 [80, 96], replicated, may hold values from -0.625 to 0.625
- bias_one: float32 [80], replicated, may hold values from -3 to 3
- hidden_weight: bfloat16 [80, 80], replicated, may hold values from -1 to 1
- bias_two: float32 [80], replicated, may hold values from -3 to 3
- out_weight: bfloat16 [96, 80], replicated, may hold values from -1 to 1
- bias_three: float32 [96], replicated, may hold values from -3 to 3
Outputs:
- latent: float32 [96, 1024], P('chan', 'slab')
Inputs may be any that keep to these rules, and one draw needn't show every extreme that they name: `send_count`: every slab has at least one live slot in each direction; some slab has all 1024 slots of its lower list live. `neighbours`: entries index the slab's point table: below 2048 own points, then 1024 slots from the slab below, then 1024 from the slab above; slot 0 of every node is an own point; nodes of the lower plane of a slab use the slots from below, those of the upper plane the slots from above, and may name dead slots.
All inputs are finite; a program needn't handle non-finite values.
Results may differ from a plain program's by a relative error of at most 0.0013.
Values may be sent and summed in bfloat16 or wider, within the bound.
No kernel may reach another device: no remote copies, remote signals or barrier semaphores. Data moves between devices by JAX's collectives and lax.ppermute only.
A program may use at most 64 MiB of HBM per device.

v0:
```python
import jax
import jax.numpy as jnp
from jax import lax
from jax.sharding import PartitionSpec as P

ZD = 2
GX = 16
GY = 4


def padded(block, sides, width):
    for axis, dim in sides:
        count = lax.axis_size(axis)
        forward = [(i, i + 1) for i in range(count - 1)]
        backward = [(target, source) for source, target in forward]
        low = lax.ppermute(
            lax.slice_in_dim(block, block.shape[dim] - width, None, axis=dim), axis, forward
        )
        high = lax.ppermute(lax.slice_in_dim(block, 0, width, axis=dim), axis, backward)
        block = jnp.concatenate([low, block, high], axis=dim)
    return block


def node_term(geom_weight, bias_one, node_ids, depth):
    along_x = ((node_ids % GX).astype(jnp.float32) + 0.5) / GX
    along_y = ((node_ids // GX % GY).astype(jnp.float32) + 0.5) / GY
    along_z = ((node_ids // (GX * GY)).astype(jnp.float32) + 0.5) / depth
    geom = geom_weight[:, 0:3].astype(jnp.float32)
    return (
        geom[:, 0:1] * along_x[None, :]
        + geom[:, 1:2] * along_y[None, :]
        + geom[:, 2:3] * along_z[None, :]
        + bias_one[:, None]
    )


def kernel_block(
    pre_table,
    value_table,
    flag_table,
    nbr,
    counts,
    node_pre,
    hidden_weight,
    bias_two,
    out_rows,
    bias_rows,
):
    nodes, slots = nbr.shape
    hidden = pre_table.shape[0]
    flat = nbr.reshape(-1)
    gathered = jnp.take(pre_table, flat, axis=1).astype(jnp.float32).reshape(hidden, nodes, slots)
    first = (
        jax.nn.gelu(gathered + node_pre[:, :, None])
        .reshape(hidden, nodes * slots)
        .astype(jnp.bfloat16)
    )
    second = jax.nn.gelu(
        jnp.dot(hidden_weight, first, preferred_element_type=jnp.float32) + bias_two[:, None]
    ).astype(jnp.bfloat16)
    kappa = jnp.dot(out_rows, second, preferred_element_type=jnp.float32) + bias_rows[:, None]
    values = jnp.take(value_table, flat, axis=1).astype(jnp.float32)
    used = (jnp.arange(slots, dtype=jnp.int32)[None, :] < counts[:, None]).astype(jnp.float32)
    flags = jnp.take(flag_table, flat).astype(jnp.float32) * used.reshape(-1)
    total = (kappa * values * flags[None, :]).reshape(out_rows.shape[0], nodes, slots).sum(axis=2)
    weight = flags.reshape(nodes, slots).sum(axis=1)
    return total / weight[None, :]


def encode(
    pre_table,
    value_table,
    flag_table,
    nbr,
    counts,
    first_id,
    depth,
    geom_weight,
    bias_one,
    hidden_weight,
    bias_two,
    out_rows,
    bias_rows,
):
    nodes = nbr.shape[0]
    block = min(128, nodes)
    blocks = nodes // block

    def one_block(index):
        start = index * block
        ids = first_id + start + jnp.arange(block, dtype=jnp.int32)
        node_pre = node_term(geom_weight, bias_one, ids, depth)
        return kernel_block(
            pre_table,
            value_table,
            flag_table,
            nbr,
            counts,
            node_pre,
            hidden_weight,
            bias_two,
            out_rows,
            bias_rows,
        )

    result = lax.map(one_block, jnp.arange(blocks, dtype=jnp.int32))
    return result.transpose(1, 0, 2).reshape(out_rows.shape[0], nodes)


def shards(
    features,
    coords,
    send_rows,
    send_count,
    neighbours,
    neighbour_count,
    geom_weight,
    feat_weight,
    bias_one,
    hidden_weight,
    bias_two,
    out_weight,
    bias_three,
):
    groups = lax.axis_size("chan")
    member = lax.axis_index("chan")
    slab_id = lax.axis_index("slab")
    depth = ZD * lax.axis_size("slab")
    own_full = lax.all_gather(features, "chan", axis=0, tiled=True)
    pre_own = (
        jnp.dot(feat_weight, own_full, preferred_element_type=jnp.float32)
        + jnp.dot(geom_weight[:, 3:6], coords, preferred_element_type=jnp.float32)
    ).astype(jnp.bfloat16)
    send = send_rows.shape[1]
    points = features.shape[1]
    hidden = pre_own.shape[0]
    chans = own_full.shape[0]
    columns = send_rows.reshape(-1)
    live = (
        (jnp.arange(send, dtype=jnp.int32)[None, :] < send_count)
        .astype(jnp.bfloat16)
        .reshape(1, 2 * send)
    )
    pre_sel = jnp.take(pre_own, columns, axis=1)
    val_sel = jnp.take(own_full, columns, axis=1)
    ones_row = jnp.ones((1, 2 * send), jnp.bfloat16)
    payload = jnp.concatenate([pre_sel, val_sel, ones_row], axis=0) * live
    extended = padded(payload, (("slab", 1),), send)
    below = extended[:, :send]
    above = extended[:, 3 * send :]
    below_pre = below[:hidden]
    above_pre = above[:hidden]
    below_vals = below[hidden : hidden + chans]
    above_vals = above[hidden : hidden + chans]
    below_flag = below[hidden + chans]
    above_flag = above[hidden + chans]
    pre_table = jnp.concatenate([pre_own, below_pre, above_pre], axis=1)
    value_table = jnp.concatenate([own_full, below_vals, above_vals], axis=1)
    flag_table = jnp.concatenate(
        [jnp.ones((points,), jnp.bfloat16), below_flag, above_flag], axis=0
    )
    per_slab = neighbours.shape[0]
    share = per_slab // groups
    start = member * share
    part_nbr = lax.dynamic_slice_in_dim(neighbours, start, share, 0)
    part_cnt = lax.dynamic_slice_in_dim(neighbour_count, start, share, 0)
    partial_value = encode(
        pre_table,
        value_table,
        flag_table,
        part_nbr,
        part_cnt,
        slab_id * per_slab + start,
        depth,
        geom_weight,
        bias_one,
        hidden_weight,
        bias_two,
        out_weight,
        bias_three,
    )
    return lax.all_to_all(partial_value, "chan", split_axis=0, concat_axis=1, tiled=True)


def solution(mesh):
    placed = (
        P("chan", "slab"),
        P(None, "slab"),
        P(None, "slab"),
        P(None, "slab"),
        P("slab", None),
        P("slab"),
        P(),
        P(),
        P(),
        P(),
        P(),
        P(),
        P(),
    )
    return jax.shard_map(
        shards, mesh=mesh, in_specs=placed, out_specs=P("chan", "slab"), check_vma=False
    )
```

profile of v0, /device:TPU:1, one launch (start us, length us, event | category | flops | bytes accessed | tf_op | source)
XLA Modules:
  0.0 116.7 jit_solution(4114827480123415698)
XLA Ops:
  0.0 0.7 compare_and_fusion.1
  0.8 0.7 fusion.37
  1.5 0.7 copy.71
  2.2 14.1 %all_gather.3 = bf16[96,2048]{1,0:T(8,128)(2,1)S(1)} all-gather(bf16[24,2048]{1,0:T(8,128)(2,1)} %param.13), channel_id=1, replica_groups=mesh['slab'=8,'chan'=4] {'chan'}, dimensions={0}, use_global_device_ids=true | all-gather | bytes 491520 | tf_op jit(solution)/shard_map/all_gather | solution.py:129
  16.3 0.3 copy.57
  16.6 0.2 fusion.59
  16.9 0.3 fusion.3
  17.2 0.3 copy.55
  17.4 6.2 %gather_fusion = bf16[2048,80]{1,0:T(8,128)(2,1)S(1)} fusion(bf16[80,2048]{0,1:T(8,128)(2,1)S(1)} %copy.55, s32[2048]{0:T(1024)S(1)} %broadcast_clamp_fusion.1), kind=kCustom, calls=%fused_computation | custom fusion | bytes 663552 | tf_op jit(solution)/shard_map/jit(_take)/gather | solution.py:144
  23.6 0.2 copy.56
  23.9 6.2 %gather_fusion.1 = bf16[2048,96]{1,0:T(8,128)(2,1)S(1)} fusion(bf16[96,2048]{0,1:T(8,128)(2,1)S(1)} %copy.57, s32[2048]{0:T(1024)S(1)} %broadcast_clamp_fusion.1), kind=kCustom, calls=%fused_computation.1 | custom fusion | bytes 794624 | tf_op jit(solution)/shard_map/jit(_take)/gather | solution.py:145
  30.0 0.2 copy.58
  30.4 0.1 pad.11.clone
  30.4 0.2 maximum_multiply_fusion
  30.7 0.1 fusion.58
  30.7 5.4 %collective-permute-start = (bf16[177,1024]{1,0:T(8,128)(2,1)S(1)}, bf16[177,1024]{1,0:T(8,128)(2,1)S(1)}, u32[]{:S(2)}, u32[]{:S(2)}) collective-permute-start(bf16[177,1024]{1,0:T(8,128)(2,1)S(1)} %get-tuple-element.33), channel_id=1, source_target_pairs={{0,4},{4,8},{8,12},{12,16},{16,20},{20,24},{24,28},{1,5},{5,9},{9,... | collective-permute-start | bytes 1087496 | tf_op jit(solution)/shard_map/ppermute | solution.py:16
  36.2 1.9 %collective-permute-start.1 = (bf16[177,1024]{1,0:T(8,128)(2,1)S(1)}, bf16[177,1024]{1,0:T(8,128)(2,1)S(1)}, u32[]{:S(2)}, u32[]{:S(2)}) collective-permute-start(bf16[177,1024]{1,0:T(8,128)(2,1)S(1)} %get-tuple-element.34), channel_id=1, source_target_pairs={{4,0},{8,4},{12,8},{16,12},{20,16},{24,20},{28,24},{5,1},{9,5},{13... | collective-permute-start | bytes 1087496 | tf_op jit(solution)/shard_map/ppermute | solution.py:19
  38.2 0.1 add_add_fusion
  38.3 0.1 dynamic_slice.10
  38.4 0.1 copy.61
  38.5 2.2 %collective-permute-done = bf16[177,1024]{1,0:T(8,128)(2,1)S(1)} collective-permute-done((bf16[177,1024]{1,0:T(8,128)(2,1)S(1)}, bf16[177,1024]{1,0:T(8,128)(2,1)S(1)}, u32[]{:S(2)}, u32[]{:S(2)}) %collective-permute-start) | collective-permute-done | bytes 362528 | tf_op jit(solution)/shard_map/ppermute | solution.py:16
  40.7 5.7 %collective-permute-done.1 = bf16[177,1024]{1,0:T(8,128)(2,1)S(1)} collective-permute-done((bf16[177,1024]{1,0:T(8,128)(2,1)S(1)}, bf16[177,1024]{1,0:T(8,128)(2,1)S(1)}, u32[]{:S(2)}, u32[]{:S(2)}) %collective-permute-start.1) | collective-permute-done | bytes 362528 | tf_op jit(solution)/shard_map/ppermute | solution.py:19
  46.4 25.6 %gather_fusion.4 = bf16[4096]{0:T(1024)(128)(2,1)S(1)} fusion(bf16[4096]{0:T(1024)(128)(2,1)S(1)} %pad_maximum_fusion.2, s32[4096]{0:T(1024)S(1)} %broadcast_clamp_fusion), kind=kCustom, calls=%fused_computation.4 | custom fusion | bytes 32768 | tf_op jit(solution)/shard_map/while/body/eval_jaxpr/jit(_take)/gather | solution.py:64
  72.1 0.2 select_reduce_fusion
  72.3 0.1 convert_select_fusion
  72.4 0.2 copy.63
  72.6 0.2 copy.64
  72.7 0.2 pad_maximum_fusion
  73.0 12.1 %gather_fusion.3 = bf16[4096,96]{1,0:T(8,128)(2,1)S(1)} fusion(bf16[96,4096]{0,1:T(8,128)(2,1)S(1)} %pad_maximum_fusion, s32[4096]{0:T(1024)S(1)} %broadcast_clamp_fusion), kind=kCustom, calls=%fused_computation.3 | custom fusion | bytes 1589248 | tf_op jit(solution)/shard_map/while/body/eval_jaxpr/jit(_take)/gather | solution.py:62
  85.1 1.2 %copy.65 = bf16[4096,96]{0,1:T(8,128)(2,1)} copy(bf16[4096,96]{1,0:T(8,128)(2,1)S(1)} %gather_fusion.3) | data formatting | bytes 1572864 | tf_op jit(solution)/shard_map/while/body/eval_jaxpr/jit(_take)/gather | solution.py:62
  86.4 0.6 copy.59
  87.1 12.1 %gather_fusion.2 = bf16[4096,80]{1,0:T(8,128)(2,1)S(1)} fusion(bf16[80,4096]{0,1:T(8,128)(2,1)S(1)} %copy.59, s32[4096]{0:T(1024)S(1)} %broadcast_clamp_fusion), kind=kCustom, calls=%fused_computation.2 | custom fusion | bytes 1327104 | tf_op jit(solution)/shard_map/while/body/eval_jaxpr/jit(_take)/gather | solution.py:52
  99.2 0.0 copy-start.8
  99.2 0.0 copy-start.10
  99.2 1.3 %copy.60 = bf16[4096,80]{0,1:T(8,128)(2,1)} copy(bf16[4096,80]{1,0:T(8,128)(2,1)S(1)} %gather_fusion.2) | data formatting | bytes 1310720 | tf_op jit(solution)/shard_map/while/body/eval_jaxpr/jit(_take)/gather | solution.py:52
  100.5 0.4 add.268
  100.9 3.2 %fusion.4 = f32[12,8,32,128]{3,1,2,0:T(8,128)S(1)} fusion(bf16[96,80]{0,1:T(8,128)(2,1)S(1)} %copy-done, bf16[80,80]{1,0:T(8,128)(2,1)S(1)} %copy-done.8, f32[4096]{0:T(1024)S(1)} %get-tuple-element.31, bf16[4096,96]{0,1:T(8,128)(2,1)} %copy.65, f32[96]{0:T(128)S(1)} %copy-done.10, pred[4096]{0:T(1024)(128)(4,1)S(1)} %get-tuple-element.32, ...), kind=kOutput, calls=%fused_computation.14 | convolution fusion | flops 124518400 | bytes 4374720 | tf_op jit(solution)/shard_map/while/body/eval_jaxpr/dot_general | solution.py:61
  104.2 0.3 copy.74
  104.5 0.5 reduce_sum.22
  105.0 0.1 copy.69
  105.0 0.1 broadcast_divide_fusion
  105.2 0.1 copy.67
  105.2 0.1 reshape.384
  105.3 9.4 %all_to_all.16 = f32[4,1,768]{2,1,0:T(1,128)S(1)} all-to-all(f32[4,1,768]{2,1,0:T(1,128)S(1)} %reshape.384), channel_id=1, replica_groups=mesh['slab'=8,'chan'=4] {'chan'}, dimensions={0} | all-to-all | bytes 24576 | tf_op jit(solution)/shard_map/all_to_all | solution.py:182
  114.7 0.5 broadcast.479
  115.2 0.7 reduce.4
  115.9 0.1 reshape.385
  116.0 0.7 all_to_all.14
  (46 shorter events, 0.4 us)
Async XLA Ops:
  0.0 100.9 %copy-start = (bf16[96,80]{0,1:T(8,128)(2,1)S(1)}, bf16[96,80]{0,1:T(8,128)(2,1)}, u32[]{:S(2)}) copy-start(bf16[96,80]{0,1:T(8,128)(2,1)} %param.24) | copy-start | bytes 46084
  0.0 16.6 %copy-start.4 = (bf16[80,96]{1,0:T(8,128)(2,1)S(1)}, bf16[80,96]{1,0:T(8,128)(2,1)}, u32[]{:S(2)}) copy-start(bf16[80,96]{1,0:T(8,128)(2,1)} %param.20) | copy-start | bytes 46084
  0.0 16.8 %copy-start.6 = (bf16[80,6]{0,1:T(8,128)(2,1)S(1)}, bf16[80,6]{0,1:T(8,128)(2,1)}, u32[]{:S(2)}) copy-start(bf16[80,6]{0,1:T(8,128)(2,1)} %param.19) | copy-start | bytes 2884
  0.0 16.8 %copy-start.5 = (bf16[3,2048]{1,0:T(4,128)(2,1)S(1)}, bf16[3,2048]{1,0:T(4,128)(2,1)}, u32[]{:S(2)}) copy-start(bf16[3,2048]{1,0:T(4,128)(2,1)} %param.14) | copy-start | bytes 36868
  30.4 7.7 %copy-start.3 = (s32[128,128]{1,0:T(8,128)S(1)}, s32[128,128]{1,0:T(8,128)}, u32[]{:S(2)}) copy-start(s32[128,128]{1,0:T(8,128)} %param.17) | copy-start | bytes 196612
  30.4 7.8 %copy-start.7 = (f32[80]{0:T(128)S(1)}, f32[80]{0:T(128)}, u32[]{:S(2)}) copy-start(f32[80]{0:T(128)} %param.21) | copy-start | bytes 964
  30.4 7.9 %copy-start.9 = (s32[128]{0:T(128)S(1)}, s32[128]{0:T(128)}, u32[]{:S(2)}) copy-start(s32[128]{0:T(128)} %param.18) | copy-start | bytes 1540
  30.7 10.0 %collective-permute-start = (bf16[177,1024]{1,0:T(8,128)(2,1)S(1)}, bf16[177,1024]{1,0:T(8,128)(2,1)S(1)}, u32[]{:S(2)}, u32[]{:S(2)}) collective-permute-start(bf16[177,1024]{1,0:T(8,128)(2,1)S(1)} %get-tuple-element.33), channel_id=1, source_target_pairs={{0,4},{4,8},{8,12},{12,16},{16,20},{20,24},{24,28},{1,5},{5,9},{9,... | collective-permute-start | bytes 1087496 | tf_op jit(solution)/shard_map/ppermute | solution.py:16
  36.2 10.2 %collective-permute-start.1 = (bf16[177,1024]{1,0:T(8,128)(2,1)S(1)}, bf16[177,1024]{1,0:T(8,128)(2,1)S(1)}, u32[]{:S(2)}, u32[]{:S(2)}) collective-permute-start(bf16[177,1024]{1,0:T(8,128)(2,1)S(1)} %get-tuple-element.34), channel_id=1, source_target_pairs={{4,0},{8,4},{12,8},{16,12},{20,16},{24,20},{28,24},{5,1},{9,5},{13... | collective-permute-start | bytes 1087496 | tf_op jit(solution)/shard_map/ppermute | solution.py:19
  40.7 31.6 %copy-start.1 = (bf16[177,1024]{1,0:T(8,128)(2,1)}, bf16[177,1024]{1,0:T(8,128)(2,1)S(1)}, u32[]{:S(2)}) copy-start(bf16[177,1024]{1,0:T(8,128)(2,1)S(1)} %collective-permute-done) | copy-start | bytes 1087492
  46.4 26.1 %copy-start.2 = (bf16[177,1024]{1,0:T(8,128)(2,1)}, bf16[177,1024]{1,0:T(8,128)(2,1)S(1)}, u32[]{:S(2)}) copy-start(bf16[177,1024]{1,0:T(8,128)(2,1)S(1)} %collective-permute-done.1) | copy-start | bytes 1087492
  85.1 1.3 %slice-start = ((bf16[177,1024]{1,0:T(8,128)(2,1)}), bf16[80,1024]{1,0:T(8,128)(2,1)S(1)}, s32[]{:S(2)}) async-start(bf16[177,1024]{1,0:T(8,128)(2,1)} %copy-done.1), calls=%async_computation.1 | async-start | bytes 327680 | tf_op jit(solution)/shard_map/slice | solution.py:151
  85.1 1.3 %slice-start.1 = ((bf16[177,1024]{1,0:T(8,128)(2,1)}), bf16[80,1024]{1,0:T(8,128)(2,1)S(1)}, s32[]{:S(2)}) async-start(bf16[177,1024]{1,0:T(8,128)(2,1)} %copy-done.2), calls=%async_computation.2 | async-start | bytes 327680 | tf_op jit(solution)/shard_map/slice | solution.py:152
  99.2 1.7 %copy-start.8 = (bf16[80,80]{1,0:T(8,128)(2,1)S(1)}, bf16[80,80]{1,0:T(8,128)(2,1)}, u32[]{:S(2)}) copy-start(bf16[80,80]{1,0:T(8,128)(2,1)} %param.22) | copy-start | bytes 38404
  99.2 1.7 %copy-start.10 = (f32[96]{0:T(128)S(1)}, f32[96]{0:T(128)}, u32[]{:S(2)}) copy-start(f32[96]{0:T(128)} %param.25) | copy-start | bytes 1156
  99.2 1.7 %copy-start.11 = (f32[80]{0:T(128)S(1)}, f32[80]{0:T(128)}, u32[]{:S(2)}) copy-start(f32[80]{0:T(128)} %param.23) | copy-start | bytes 964
where the time goes:
time: 117 us
  local copies, waits for them, and re-layouts  70.1 us (60%)
  blocking collectives  23.4 us (20%)
  waiting for transfers between devices  7.85 us (7%)
  starting transfers between devices  7.34 us (6%)
  matrix products  3.76 us (3%)
  other arithmetic  3.72 us (3%)
    gather x1, local copies, waits for them, and re-layouts, kernel_block(): flags = jnp.take(flag_table, flat).astype(jnp.float32) * used.reshape(-1)  25.6 us
    all_gather x1, blocking collectives, shards(): own_full = lax.all_gather(features, 'chan', axis=0, tiled=True)  14.1 us
    gather x2, local copies, waits for them, and re-layouts, kernel_block(): jnp.take(pre_table, flat, axis=1).astype(jnp.float32)  13.4 us
    gather x2, local copies, waits for them, and re-layouts, kernel_block(): values = jnp.take(value_table, flat, axis=1).astype(jnp.float32)  13.4 us
    all_to_all x1, blocking collectives, shards(): lax.all_to_all(partial_value, 'chan', split_axis=0, concat_axis=1, tiled=...  9.35 us
    gather x2, local copies, waits for them, and re-layouts, shards(): val_sel = jnp.take(own_full, columns, axis=1)  6.4 us
    gather x2, local copies, waits for them, and re-layouts, shards(): pre_sel = jnp.take(pre_own, columns, axis=1)  6.4 us
    ppermute x1, waiting for transfers between devices, padded(): lax.ppermute(lax.slice_in_dim(block, 0, width, axis=dim), axis, backward)  5.67 us
  transfers between devices with their start and end apart: 2, of which 2 were waited for; matrix products, arithmetic and copies ran while one was open for 0% of the time, Pallas kernels for 0%

commit v1 on v0

--- a/solution.py
+++ b/solution.py
@@ -179,7 +179,12 @@
         out_weight,
         bias_three,
     )
-    return lax.all_to_all(partial_value, "chan", split_axis=0, concat_axis=1, tiled=True)
+    return jnp.concatenate(
+        lax.all_to_all(
+            jnp.stack(jnp.split(partial_value, lax.axis_size("chan"), axis=0)), "chan", 0, 0
+        ),
+        axis=1,
+    )
 
 
 def solution(mesh):

time: 117 us -> 117 us (level)
  no operation moved by 1% of the time
where the time goes in v1:
time: 117 us; the launch traced here: 116 us
  local copies, waits for them, and re-layouts  70 us (60%)
  blocking collectives  23.4 us (20%)
  waiting for transfers between devices  7.85 us (7%)
  starting transfers between devices  7.34 us (6%)
  matrix products  3.76 us (3%)
  other arithmetic  3.63 us (3%)
    gather x1, local copies, waits for them, and re-layouts, kernel_block(): flags = jnp.take(flag_table, flat).astype(jnp.float32) * used.reshape(-1)  25.6 us
    all_gather x1, blocking collectives, shards(): own_full = lax.all_gather(features, 'chan', axis=0, tiled=True)  14.1 us
    gather x2, local copies, waits for them, and re-layouts, kernel_block(): values = jnp.take(value_table, flat, axis=1).astype(jnp.float32)  13.4 us
    gather x2, local copies, waits for them, and re-layouts, kernel_block(): jnp.take(pre_table, flat, axis=1).astype(jnp.float32)  13.4 us
    all_to_all x1, blocking collectives, shards(): lax.all_to_all(jnp.stack(jnp.split(partial_value, lax.axis_size('chan'),...  9.35 us
    gather x2, local copies, waits for them, and re-layouts, shards(): val_sel = jnp.take(own_full, columns, axis=1)  6.4 us
    gather x2, local copies, waits for them, and re-layouts, shards(): pre_sel = jnp.take(pre_own, columns, axis=1)  6.4 us
    ppermute x1, waiting for transfers between devices, padded(): lax.ppermute(lax.slice_in_dim(block, 0, width, axis=dim), axis, backward)  5.67 us
  transfers between devices with their start and end apart: 2, of which 2 were waited for; matrix products, arithmetic and copies ran while one was open for 0% of the time, Pallas kernels for 0%

profile of v1, /device:TPU:1, one launch (start us, length us, event | category | flops | bytes accessed | tf_op | source)
XLA Modules:
  0.0 116.5 jit_solution(12410105156077738369)
XLA Ops:
  0.0 0.7 compare_and_fusion.1
  0.8 0.7 fusion.37
  1.5 0.7 copy.72
  2.2 14.1 %all_gather.3 = bf16[96,2048]{1,0:T(8,128)(2,1)S(1)} all-gather(bf16[24,2048]{1,0:T(8,128)(2,1)} %param.13), channel_id=1, replica_groups=mesh['slab'=8,'chan'=4] {'chan'}, dimensions={0}, use_global_device_ids=true | all-gather | bytes 491520 | tf_op jit(solution)/shard_map/all_gather | solution.py:129
  16.3 0.3 copy.61
  16.6 0.2 fusion.59
  16.9 0.3 fusion.3
  17.2 0.3 copy.59
  17.4 6.2 %gather_fusion = bf16[2048,80]{1,0:T(8,128)(2,1)S(1)} fusion(bf16[80,2048]{0,1:T(8,128)(2,1)S(1)} %copy.59, s32[2048]{0:T(1024)S(1)} %broadcast_clamp_fusion.1), kind=kCustom, calls=%fused_computation | custom fusion | bytes 663552 | tf_op jit(solution)/shard_map/jit(_take)/gather | solution.py:144
  23.6 0.2 copy.60
  23.9 6.2 %gather_fusion.1 = bf16[2048,96]{1,0:T(8,128)(2,1)S(1)} fusion(bf16[96,2048]{0,1:T(8,128)(2,1)S(1)} %copy.61, s32[2048]{0:T(1024)S(1)} %broadcast_clamp_fusion.1), kind=kCustom, calls=%fused_computation.1 | custom fusion | bytes 794624 | tf_op jit(solution)/shard_map/jit(_take)/gather | solution.py:145
  30.0 0.2 copy.62
  30.4 0.1 pad.15.clone
  30.4 0.2 maximum_multiply_fusion
  30.7 0.1 fusion.58
  30.7 5.4 %collective-permute-start = (bf16[177,1024]{1,0:T(8,128)(2,1)S(1)}, bf16[177,1024]{1,0:T(8,128)(2,1)S(1)}, u32[]{:S(2)}, u32[]{:S(2)}) collective-permute-start(bf16[177,1024]{1,0:T(8,128)(2,1)S(1)} %get-tuple-element.33), channel_id=1, source_target_pairs={{0,4},{4,8},{8,12},{12,16},{16,20},{20,24},{24,28},{1,5},{5,9},{9,... | collective-permute-start | bytes 1087496 | tf_op jit(solution)/shard_map/ppermute | solution.py:16
  36.2 1.9 %collective-permute-start.1 = (bf16[177,1024]{1,0:T(8,128)(2,1)S(1)}, bf16[177,1024]{1,0:T(8,128)(2,1)S(1)}, u32[]{:S(2)}, u32[]{:S(2)}) collective-permute-start(bf16[177,1024]{1,0:T(8,128)(2,1)S(1)} %get-tuple-element.34), channel_id=1, source_target_pairs={{4,0},{8,4},{12,8},{16,12},{20,16},{24,20},{28,24},{5,1},{9,5},{13... | collective-permute-start | bytes 1087496 | tf_op jit(solution)/shard_map/ppermute | solution.py:19
  38.2 0.1 add_add_fusion
  38.3 0.1 dynamic_slice.10
  38.4 0.1 copy.65
  38.5 2.2 %collective-permute-done = bf16[177,1024]{1,0:T(8,128)(2,1)S(1)} collective-permute-done((bf16[177,1024]{1,0:T(8,128)(2,1)S(1)}, bf16[177,1024]{1,0:T(8,128)(2,1)S(1)}, u32[]{:S(2)}, u32[]{:S(2)}) %collective-permute-start) | collective-permute-done | bytes 362528 | tf_op jit(solution)/shard_map/ppermute | solution.py:16
  40.7 5.7 %collective-permute-done.1 = bf16[177,1024]{1,0:T(8,128)(2,1)S(1)} collective-permute-done((bf16[177,1024]{1,0:T(8,128)(2,1)S(1)}, bf16[177,1024]{1,0:T(8,128)(2,1)S(1)}, u32[]{:S(2)}, u32[]{:S(2)}) %collective-permute-start.1) | collective-permute-done | bytes 362528 | tf_op jit(solution)/shard_map/ppermute | solution.py:19
  46.4 25.6 %gather_fusion.4 = bf16[4096]{0:T(1024)(128)(2,1)S(1)} fusion(bf16[4096]{0:T(1024)(128)(2,1)S(1)} %pad_maximum_fusion.3, s32[4096]{0:T(1024)S(1)} %broadcast_clamp_fusion), kind=kCustom, calls=%fused_computation.4 | custom fusion | bytes 32768 | tf_op jit(solution)/shard_map/while/body/eval_jaxpr/jit(_take)/gather | solution.py:64
  72.1 0.2 select_reduce_fusion
  72.3 0.1 convert_select_fusion
  72.4 0.2 copy.67
  72.6 0.2 copy.68
  72.7 0.2 pad_maximum_fusion
  73.0 12.1 %gather_fusion.3 = bf16[4096,96]{1,0:T(8,128)(2,1)S(1)} fusion(bf16[96,4096]{0,1:T(8,128)(2,1)S(1)} %pad_maximum_fusion, s32[4096]{0:T(1024)S(1)} %broadcast_clamp_fusion), kind=kCustom, calls=%fused_computation.3 | custom fusion | bytes 1589248 | tf_op jit(solution)/shard_map/while/body/eval_jaxpr/jit(_take)/gather | solution.py:62
  85.1 0.0 slice-start
  85.1 0.0 slice-start.1
  85.1 1.3 %copy.69 = bf16[4096,96]{0,1:T(8,128)(2,1)} copy(bf16[4096,96]{1,0:T(8,128)(2,1)S(1)} %gather_fusion.3) | data formatting | bytes 1572864 | tf_op jit(solution)/shard_map/while/body/eval_jaxpr/jit(_take)/gather | solution.py:62
  86.4 0.6 copy.63
  87.1 12.1 %gather_fusion.2 = bf16[4096,80]{1,0:T(8,128)(2,1)S(1)} fusion(bf16[80,4096]{0,1:T(8,128)(2,1)S(1)} %copy.63, s32[4096]{0:T(1024)S(1)} %broadcast_clamp_fusion), kind=kCustom, calls=%fused_computation.2 | custom fusion | bytes 1327104 | tf_op jit(solution)/shard_map/while/body/eval_jaxpr/jit(_take)/gather | solution.py:52
  99.2 0.0 copy-start.8
  99.3 0.0 copy-start.10
  99.3 0.0 copy-start.11
  99.3 1.3 %copy.64 = bf16[4096,80]{0,1:T(8,128)(2,1)} copy(bf16[4096,80]{1,0:T(8,128)(2,1)S(1)} %gather_fusion.2) | data formatting | bytes 1310720 | tf_op jit(solution)/shard_map/while/body/eval_jaxpr/jit(_take)/gather | solution.py:52
  100.5 0.4 add.268
  101.0 3.2 %fusion.4 = f32[12,8,32,128]{3,1,2,0:T(8,128)S(1)} fusion(bf16[96,80]{0,1:T(8,128)(2,1)S(1)} %copy-done, bf16[80,80]{1,0:T(8,128)(2,1)S(1)} %copy-done.8, f32[4096]{0:T(1024)S(1)} %get-tuple-element.31, bf16[4096,96]{0,1:T(8,128)(2,1)} %copy.69, f32[96]{0:T(128)S(1)} %copy-done.10, pred[4096]{0:T(1024)(128)(4,1)S(1)} %get-tuple-element.32, ...), kind=kOutput, calls=%fused_computation.14 | convolution fusion | flops 124518400 | bytes 4374720 | tf_op jit(solution)/shard_map/while/body/eval_jaxpr/dot_general | solution.py:61
  104.2 0.3 copy.75
  104.5 0.5 reduce_sum.20
  105.1 0.1 reshape.383
  105.1 9.3 %all_to_all.5 = f32[4,1,768]{2,1,0:T(1,128)S(1)} all-to-all(f32[4,1,768]{2,1,0:T(1,128)S(1)} %reshape.383), channel_id=1, replica_groups=mesh['slab'=8,'chan'=4] {'chan'}, dimensions={0} | all-to-all | bytes 24576 | tf_op jit(solution)/shard_map/all_to_all | solution.py:183
  114.5 0.5 broadcast.477
  115.0 0.7 reduce.4
  115.7 0.1 reshape.384
  115.8 0.7 reshape.338
  (46 shorter events, 0.4 us)
Async XLA Ops:
  0.0 101.0 %copy-start = (bf16[96,80]{0,1:T(8,128)(2,1)S(1)}, bf16[96,80]{0,1:T(8,128)(2,1)}, u32[]{:S(2)}) copy-start(bf16[96,80]{0,1:T(8,128)(2,1)} %param.24) | copy-start | bytes 46084
  0.0 16.6 %copy-start.4 = (bf16[80,96]{1,0:T(8,128)(2,1)S(1)}, bf16[80,96]{1,0:T(8,128)(2,1)}, u32[]{:S(2)}) copy-start(bf16[80,96]{1,0:T(8,128)(2,1)} %param.20) | copy-start | bytes 46084
  0.0 16.8 %copy-start.6 = (bf16[80,6]{0,1:T(8,128)(2,1)S(1)}, bf16[80,6]{0,1:T(8,128)(2,1)}, u32[]{:S(2)}) copy-start(bf16[80,6]{0,1:T(8,128)(2,1)} %param.19) | copy-start | bytes 2884
  0.0 16.8 %copy-start.5 = (bf16[3,2048]{1,0:T(4,128)(2,1)S(1)}, bf16[3,2048]{1,0:T(4,128)(2,1)}, u32[]{:S(2)}) copy-start(bf16[3,2048]{1,0:T(4,128)(2,1)} %param.14) | copy-start | bytes 36868
  30.4 7.7 %copy-start.3 = (s32[128,128]{1,0:T(8,128)S(1)}, s32[128,128]{1,0:T(8,128)}, u32[]{:S(2)}) copy-start(s32[128,128]{1,0:T(8,128)} %param.17) | copy-start | bytes 196612
  30.4 7.8 %copy-start.7 = (f32[80]{0:T(128)S(1)}, f32[80]{0:T(128)}, u32[]{:S(2)}) copy-start(f32[80]{0:T(128)} %param.21) | copy-start | bytes 964
  30.4 7.9 %copy-start.9 = (s32[128]{0:T(128)S(1)}, s32[128]{0:T(128)}, u32[]{:S(2)}) copy-start(s32[128]{0:T(128)} %param.18) | copy-start | bytes 1540
  30.7 10.0 %collective-permute-start = (bf16[177,1024]{1,0:T(8,128)(2,1)S(1)}, bf16[177,1024]{1,0:T(8,128)(2,1)S(1)}, u32[]{:S(2)}, u32[]{:S(2)}) collective-permute-start(bf16[177,1024]{1,0:T(8,128)(2,1)S(1)} %get-tuple-element.33), channel_id=1, source_target_pairs={{0,4},{4,8},{8,12},{12,16},{16,20},{20,24},{24,28},{1,5},{5,9},{9,... | collective-permute-start | bytes 1087496 | tf_op jit(solution)/shard_map/ppermute | solution.py:16
  36.2 10.2 %collective-permute-start.1 = (bf16[177,1024]{1,0:T(8,128)(2,1)S(1)}, bf16[177,1024]{1,0:T(8,128)(2,1)S(1)}, u32[]{:S(2)}, u32[]{:S(2)}) collective-permute-start(bf16[177,1024]{1,0:T(8,128)(2,1)S(1)} %get-tuple-element.34), channel_id=1, source_target_pairs={{4,0},{8,4},{12,8},{16,12},{20,16},{24,20},{28,24},{5,1},{9,5},{13... | collective-permute-start | bytes 1087496 | tf_op jit(solution)/shard_map/ppermute | solution.py:19
  40.7 31.6 %copy-start.1 = (bf16[177,1024]{1,0:T(8,128)(2,1)}, bf16[177,1024]{1,0:T(8,128)(2,1)S(1)}, u32[]{:S(2)}) copy-start(bf16[177,1024]{1,0:T(8,128)(2,1)S(1)} %collective-permute-done) | copy-start | bytes 1087492
  46.4 26.1 %copy-start.2 = (bf16[177,1024]{1,0:T(8,128)(2,1)}, bf16[177,1024]{1,0:T(8,128)(2,1)S(1)}, u32[]{:S(2)}) copy-start(bf16[177,1024]{1,0:T(8,128)(2,1)S(1)} %collective-permute-done.1) | copy-start | bytes 1087492
  85.1 1.3 %slice-start = ((bf16[177,1024]{1,0:T(8,128)(2,1)}), bf16[80,1024]{1,0:T(8,128)(2,1)S(1)}, s32[]{:S(2)}) async-start(bf16[177,1024]{1,0:T(8,128)(2,1)} %copy-done.1), calls=%async_computation.1 | async-start | bytes 327680 | tf_op jit(solution)/shard_map/slice | solution.py:151
  85.1 1.3 %slice-start.1 = ((bf16[177,1024]{1,0:T(8,128)(2,1)}), bf16[80,1024]{1,0:T(8,128)(2,1)S(1)}, s32[]{:S(2)}) async-start(bf16[177,1024]{1,0:T(8,128)(2,1)} %copy-done.2), calls=%async_computation.2 | async-start | bytes 327680 | tf_op jit(solution)/shard_map/slice | solution.py:152
  99.2 1.7 %copy-start.8 = (bf16[80,80]{1,0:T(8,128)(2,1)S(1)}, bf16[80,80]{1,0:T(8,128)(2,1)}, u32[]{:S(2)}) copy-start(bf16[80,80]{1,0:T(8,128)(2,1)} %param.22) | copy-start | bytes 38404
  99.3 1.7 %copy-start.10 = (f32[96]{0:T(128)S(1)}, f32[96]{0:T(128)}, u32[]{:S(2)}) copy-start(f32[96]{0:T(128)} %param.25) | copy-start | bytes 1156
  99.3 1.7 %copy-start.11 = (f32[80]{0:T(128)S(1)}, f32[80]{0:T(128)}, u32[]{:S(2)}) copy-start(f32[80]{0:T(128)} %param.23) | copy-start | bytes 964
